TPU v7x, 512 devices: a whole 4x8x8 slice. The times are simulated.
512 devices in a mesh: cells: 64 (over x, y, z_lo), src: 8 (over z_hi, core).
Axes of the slice: x: 4, y: 8, z: 8 (z_hi: 4, z_lo: 2; z = z_hi * 2 + z_lo), core: 2. Of those that a mesh axis runs over, the one named last changes fastest.
Arguments:
- conductivity: float32 [256, 1024], P('cells'), may hold values from 0.2 to 5
- prev_fields: bfloat16 [1024, 256, 1024], P('src', 'cells'), may hold values from -6 to 6
- electrodes: int32 [1024, 2], P('src'), may hold values from 0 to 262143, as said below
- data_weight: bfloat16 [1024, 1024], replicated, may hold values from -3 to 4
Outputs:
- potentials: bfloat16 [1024, 256, 1024], P('src', 'cells')
- gradient: float32 [256, 1024], P('cells', 'src')
Inputs may be any that keep to these rules, and one draw needn't show every extreme that they name: `electrodes`: in each row the two cells differ.
All inputs are finite; a program needn't handle non-finite values.
Results may differ from a plain program's by a relative error of at most 0.0034.
Values may be sent and summed in bfloat16 or wider, within the bound.
A program may use at most 64 MiB of HBM per device.

v0:
```python
import jax
import jax.numpy as jnp
from jax import lax
from jax.sharding import PartitionSpec as P

NY = 32
ITERS = 2


relaxation = 2.0 / 3.0
current = 4.0


def with_halo(block, sides, width):
    for axis, dim in sides:
        count = lax.axis_size(axis)
        forward = [(i, i + 1) for i in range(count - 1)]
        backward = [(target, source) for source, target in forward]
        low = lax.ppermute(
            lax.slice_in_dim(block, block.shape[dim] - width, None, axis=dim), axis, forward
        )
        high = lax.ppermute(lax.slice_in_dim(block, 0, width, axis=dim), axis, backward)
        block = jnp.concatenate([low, block, high], axis=dim)
    return block


def shifted_2(value, axis, steps):
    count = lax.axis_size(axis)
    initial, last = (max(0, -steps), min(count, count - steps))
    return lax.ppermute(value, axis, [(source, source + steps) for source in range(initial, last)])


def shift_last(values, offset):
    if offset > 0:
        padding = jnp.zeros(values.shape[:-1] + (offset,), values.dtype)
        return jnp.concatenate([values[..., offset:], padding], axis=-1)
    padding = jnp.zeros(values.shape[:-1] + (-offset,), values.dtype)
    return jnp.concatenate([padding, values[..., :offset]], axis=-1)


def column_masks(length, row_len):
    column = jnp.arange(length, dtype=jnp.int32) % row_len
    return ((column != row_len - 1).astype(jnp.float32), (column != 0).astype(jnp.float32))


def coefficients(sigma_pad, row_len):
    sigma = sigma_pad[1:-1]
    upper_mask, lower_mask = column_masks(sigma.shape[-1], row_len)
    z_plus = 0.5 * (sigma + sigma_pad[2:])
    z_minus = 0.5 * (sigma + sigma_pad[:-2])
    y_plus = 0.5 * (sigma + shift_last(sigma, 1) * upper_mask)
    y_minus = 0.5 * (sigma + shift_last(sigma, -1) * lower_mask)
    x_plus = 0.5 * (sigma + shift_last(sigma, row_len))
    x_minus = 0.5 * (sigma + shift_last(sigma, -row_len))
    diagonal = z_plus + z_minus + y_plus + y_minus + x_plus + x_minus
    return (z_plus, z_minus, y_plus, y_minus, x_plus, x_minus, diagonal, upper_mask, lower_mask)


def relax(fields_pad, source, coeffs, row_len):
    z_plus, z_minus, y_plus, y_minus, x_plus, x_minus, diagonal, upper_mask, lower_mask = coeffs
    fields = fields_pad[:, 1:-1]
    applied = diagonal * fields - z_plus * fields_pad[:, 2:] - z_minus * fields_pad[:, :-2]
    applied = (
        applied
        - y_plus * (shift_last(fields, 1) * upper_mask)
        - y_minus * (shift_last(fields, -1) * lower_mask)
    )
    applied = (
        applied - x_plus * shift_last(fields, row_len) - x_minus * shift_last(fields, -row_len)
    )
    return fields + relaxation * (source - applied) / diagonal


def differences(planes, above, beside, row_len):
    upper_mask, lower_mask = column_masks(planes.shape[-1], row_len)
    along_x = jnp.concatenate([planes[..., row_len:], beside], axis=-1)
    along_y = shift_last(planes, 1) * upper_mask
    along_z = jnp.concatenate([planes[:, 1:], above], axis=1)
    return tuple(
        ((shifted - planes).astype(jnp.bfloat16) for shifted in (along_x, along_y, along_z))
    )


def weigh(diffs, data_weight):
    count = data_weight.shape[0]
    total = jnp.zeros(diffs[0].shape[1:], jnp.float32)
    for block in diffs:
        flat = block.reshape(count, -1)
        mixed = jnp.dot(data_weight, flat, preferred_element_type=jnp.float32)
        total = total + jnp.sum(flat.astype(jnp.float32) * mixed, axis=0).reshape(total.shape)
    return total / count


def make_source(electrodes, first_cell, local_sources, extent, plane_cells):
    cell_ids = first_cell + jnp.arange(extent * plane_cells, dtype=jnp.int32)
    source = current * (
        (cell_ids[None, :] == electrodes[:, 0:1]).astype(jnp.float32)
        - (cell_ids[None, :] == electrodes[:, 1:2]).astype(jnp.float32)
    )
    return source.reshape(local_sources, extent, plane_cells)


def body(conductivity, prev_fields, electrodes, data_weight):
    local_sources, depth, plane_cells = prev_fields.shape
    sigma_pad = with_halo(conductivity, (("cells", 0),), 1)
    coeffs = coefficients(sigma_pad, NY)
    source = make_source(
        electrodes,
        lax.axis_index("cells") * (depth * plane_cells),
        local_sources,
        depth,
        plane_cells,
    )
    fields = prev_fields.astype(jnp.float32)
    for sweep in range(ITERS):
        fields_pad = with_halo(fields, (("cells", 1),), 1)
        fields = relax(fields_pad, source, coeffs, NY)
    potentials = fields.astype(jnp.bfloat16)
    blocks = lax.all_to_all(potentials, "src", split_axis=2, concat_axis=0, tiled=True)
    beside = shifted_2(blocks[:, :, :NY], "src", -1)
    above = shifted_2(blocks[:, 0], "cells", -1)
    diffs = differences(
        blocks.astype(jnp.float32),
        above.astype(jnp.float32)[:, None],
        beside.astype(jnp.float32),
        NY,
    )
    gradient = weigh(diffs, data_weight)
    return (potentials, gradient)


def solution(mesh):
    placed = (P("cells", None), P("src", "cells", None), P("src", None), P())
    return jax.shard_map(
        body,
        mesh=mesh,
        in_specs=placed,
        out_specs=(P("src", "cells", None), P("cells", "src")),
        check_vma=False,
    )
```

profile of v0, /device:TPU:7, one launch (start us, length us, event | category | flops | bytes accessed | tf_op | source)
XLA Modules:
  0.0 145.9 jit_solution(6298374925849817451)
XLA Ops:
  0.6 0.9 fusion.52
  1.5 7.2 %collective-permute-start = (f32[1,1024]{1,0:T(1,128)S(1)}, f32[1,1024]{1,0:T(1,128)S(1)}, u32[]{:S(2)}, u32[]{:S(2)}) collective-permute-start(f32[1,1024]{1,0:T(1,128)S(1)} %get-tuple-element.34), channel_id=1, source_target_pairs={{8,0},{16,8},{24,16},{32,24},{40,32},{48,40},{56,48},{64,56},{72,6... | collective-permute-start | bytes 12296 | tf_op jit(solution)/shard_map/ppermute | solution.py:22
  8.7 1.9 %collective-permute-start.1 = (f32[1,1024]{1,0:T(1,128)S(1)}, f32[1,1024]{1,0:T(1,128)S(1)}, u32[]{:S(2)}, u32[]{:S(2)}) collective-permute-start(f32[1,1024]{1,0:T(1,128)S(1)} %get-tuple-element.33), channel_id=1, source_target_pairs={{0,8},{8,16},{16,24},{24,32},{32,40},{40,48},{48,56},{56,64},{64,7... | collective-permute-start | bytes 12296 | tf_op jit(solution)/shard_map/ppermute | solution.py:19
  10.7 1.6 %copy_convert_fusion = f32[128,4,1024]{2,0,1:T(8,128)S(1)} fusion(bf16[128,4,1024]{2,1,0:T(4,128)(2,1)} %param.5), kind=kLoop, calls=%fused_computation.44 | loop fusion | flops 524288 | bytes 3145728 | tf_op jit(solution)/shard_map/convert_element_type | solution.py:114
  12.3 1.2 fusion.49
  13.5 6.4 %collective-permute-start.2 = (f32[128,1,1024]{2,0,1:T(8,128)}, f32[128,1,1024]{2,0,1:T(8,128)S(1)}, u32[]{:S(2)}, u32[]{:S(2)}) collective-permute-start(f32[128,1,1024]{2,0,1:T(8,128)} %get-tuple-element.25), channel_id=1, source_target_pairs={{8,0},{16,8},{24,16},{32,24},{40,32},{48,40},{56,48},{64,56},{72,6... | collective-permute-start | bytes 1572872 | tf_op jit(solution)/shard_map/ppermute | solution.py:22
  19.8 1.9 %collective-permute-start.3 = (f32[128,1,1024]{2,0,1:T(8,128)}, f32[128,1,1024]{2,0,1:T(8,128)S(1)}, u32[]{:S(2)}, u32[]{:S(2)}) collective-permute-start(f32[128,1,1024]{2,0,1:T(8,128)} %get-tuple-element.26), channel_id=1, source_target_pairs={{0,8},{8,16},{16,24},{24,32},{32,40},{40,48},{48,56},{56,64},{64,7... | collective-permute-start | bytes 1572872 | tf_op jit(solution)/shard_map/ppermute | solution.py:19
  21.9 2.8 %fusion.47 = (f32[128,4,1023]{2,0,1:T(8,128)}, f32[128,4,1023]{2,0,1:T(8,128)}) fusion(f32[128,4,1024]{2,0,1:T(8,128)S(1)} %copy_convert_fusion), kind=kLoop, calls=%fused_computation.77 | loop fusion | bytes 8380416 | tf_op jit(solution)/shard_map/slice | solution.py:36
  24.7 2.8 %fusion.48 = (f32[128,4,992]{2,0,1:T(8,128)}, f32[128,4,992]{2,0,1:T(8,128)}) fusion(f32[128,4,1024]{2,0,1:T(8,128)S(1)} %copy_convert_fusion), kind=kLoop, calls=%fused_computation.78 | loop fusion | bytes 8126464 | tf_op jit(solution)/shard_map/slice | solution.py:36
  27.7 2.5 %collective-permute-done.2 = f32[128,1,1024]{2,0,1:T(8,128)S(1)} collective-permute-done((f32[128,1,1024]{2,0,1:T(8,128)}, f32[128,1,1024]{2,0,1:T(8,128)S(1)}, u32[]{:S(2)}, u32[]{:S(2)}) %collective-permute-start.2) | collective-permute-done | bytes 524320 | tf_op jit(solution)/shard_map/ppermute | solution.py:22
  30.2 8.4 %collective-permute-done.3 = f32[128,1,1024]{2,0,1:T(8,128)S(1)} collective-permute-done((f32[128,1,1024]{2,0,1:T(8,128)}, f32[128,1,1024]{2,0,1:T(8,128)S(1)}, u32[]{:S(2)}, u32[]{:S(2)}) %collective-permute-start.3) | collective-permute-done | bytes 524320 | tf_op jit(solution)/shard_map/ppermute | solution.py:19
  38.6 6.2 %fusion.23 = f32[128,4,1024]{2,0,1:T(8,128)S(1)} fusion(f32[128,4,1024]{2,0,1:T(8,128)} %copy-done.1, f32[128,1,1024]{2,0,1:T(8,128)S(1)} %collective-permute-done.3, f32[128,1,1024]{2,0,1:T(8,128)S(1)} %collective-permute-done.2, f32[128,4,992]{2,0,1:T(8,128)} %get-tuple-element.24, f32[128,4,992]{2,0,1:T(8,128)} %get-tuple-element.23, ...), kind=kLoop, calls=%fused_computation.28 | loop fusion | flops 14155776 | bytes 13636608 | tf_op jit(solution)/shard_map/add | solution.py:71
  45.0 10.2 %collective-permute-start.4 = (f32[128,1,1024]{2,0,1:T(8,128)S(1)}, f32[128,1,1024]{2,0,1:T(8,128)S(1)}, u32[]{:S(2)}, u32[]{:S(2)}) collective-permute-start(f32[128,1,1024]{2,0,1:T(8,128)S(1)} %get-tuple-element.15), channel_id=1, source_target_pairs={{8,0},{16,8},{24,16},{32,24},{40,32},{48,40},{56,48},{64,56},{72,6... | collective-permute-start | bytes 1572872 | tf_op jit(solution)/shard_map/ppermute | solution.py:22
  55.1 1.9 %collective-permute-start.5 = (f32[128,1,1024]{2,0,1:T(8,128)S(1)}, f32[128,1,1024]{2,0,1:T(8,128)S(1)}, u32[]{:S(2)}, u32[]{:S(2)}) collective-permute-start(f32[128,1,1024]{2,0,1:T(8,128)S(1)} %get-tuple-element.16), channel_id=1, source_target_pairs={{0,8},{8,16},{16,24},{24,32},{32,40},{40,48},{48,56},{56,64},{64,7... | collective-permute-start | bytes 1572872 | tf_op jit(solution)/shard_map/ppermute | solution.py:19
  57.9 0.8 fusion.46
  58.8 7.0 %collective-permute-done.4 = f32[128,1,1024]{2,0,1:T(8,128)S(1)} collective-permute-done((f32[128,1,1024]{2,0,1:T(8,128)S(1)}, f32[128,1,1024]{2,0,1:T(8,128)S(1)}, u32[]{:S(2)}, u32[]{:S(2)}) %collective-permute-start.4) | collective-permute-done | bytes 524320 | tf_op jit(solution)/shard_map/ppermute | solution.py:22
  65.8 6.9 %collective-permute-done.5 = f32[128,1,1024]{2,0,1:T(8,128)S(1)} collective-permute-done((f32[128,1,1024]{2,0,1:T(8,128)S(1)}, f32[128,1,1024]{2,0,1:T(8,128)S(1)}, u32[]{:S(2)}, u32[]{:S(2)}) %collective-permute-start.5) | collective-permute-done | bytes 524320 | tf_op jit(solution)/shard_map/ppermute | solution.py:19
  72.7 2.8 %fusion.29 = bf16[128,4,1024]{2,0,1:T(8,128)(2,1)S(1)} fusion(f32[128,4,1024]{2,0,1:T(8,128)S(1)} %fusion.23, f32[128,4,992]{2,0,1:T(8,128)S(1)} %get-tuple-element.20, f32[128,4,992]{2,0,1:T(8,128)S(1)} %get-tuple-element.19, f32[128,4,1023]{2,0,1:T(8,128)S(1)} %get-tuple-element.18, f32[128,4,1023]{2,0,1:T(8,128)S(1)} %get-tuple-element.17, ...), kind=kLoop, calls=%fused_computation.42 | loop fusion | flops 14680064 | bytes 12588032 | tf_op jit(solution)/shard_map/convert_element_type | solution.py:118
  75.5 1.4 copy.12
  77.0 11.0 %all-to-all-start = ((bf16[128,4,1024]{0,1,2:T(4,128)(2,1)}), bf16[128,4,1024]{0,1,2:T(4,128)(2,1)}, u32[]{:S(2)}, u32[]{:S(2)}) async-start(bf16[128,4,1024]{0,1,2:T(4,128)(2,1)} %copy.12), calls=%async_computation | async-start | bytes 2097152 | tf_op jit(solution)/shard_map/all_to_all | solution.py:119
  88.0 1.8 %copy.14 = bf16[128,4,1024]{2,1,0:T(4,128)(2,1)} copy(bf16[128,4,1024]{2,0,1:T(8,128)(2,1)S(1)} %fusion.29) | data formatting | bytes 2097152
  89.8 20.2 %all-to-all-done = bf16[128,4,1024]{0,1,2:T(4,128)(2,1)} async-done(((bf16[128,4,1024]{0,1,2:T(4,128)(2,1)}), bf16[128,4,1024]{0,1,2:T(4,128)(2,1)}, u32[]{:S(2)}, u32[]{:S(2)}) %all-to-all-start) | async-done | bytes 1048608 | tf_op jit(solution)/shard_map/all_to_all | solution.py:119
  110.0 3.6 %fusion.41 = (f32[8,128,4,128]{1,0,3,2:T(8,128)}, bf16[8,128,4,128]{1,0,3,2:T(8,128)(2,1)}) fusion(bf16[128,4,8,128]{0,1,3,2:T(4,128)(2,1)} %bitcast.2), kind=kLoop, calls=%fused_computation.73 | loop fusion | flops 524288 | bytes 4194304 | tf_op jit(solution)/shard_map/convert_element_type | solution.py:123
  113.6 1.5 %all_to_all.16 = bf16[1024,4,128]{0,2,1:T(8,128)(2,1)S(1)} reshape(bf16[8,128,4,128]{1,0,3,2:T(8,128)(2,1)} %get-tuple-element.28) | data formatting | bytes 2097152 | tf_op jit(solution)/shard_map/all_to_all | solution.py:119
  115.8 15.4 %collective-permute-start.7 = (bf16[1024,128]{0,1:T(8,128)(2,1)S(1)}, bf16[1024,128]{0,1:T(8,128)(2,1)S(1)}, u32[]{:S(2)}, u32[]{:S(2)}) collective-permute-start(bf16[1024,128]{0,1:T(8,128)(2,1)S(1)} %slice_bitcast_fusion), channel_id=1, source_target_pairs={{8,0},{16,8},{24,16},{32,24},{40,32},{48,40},{56,48},{64,56},{72,6... | collective-permute-start | bytes 786440 | tf_op jit(solution)/shard_map/ppermute | solution.py:30
  131.2 3.0 %collective-permute-start.6 = (bf16[1024,4,32]{0,2,1:T(8,128)(2,1)S(1)}, bf16[1024,4,32]{0,2,1:T(8,128)(2,1)S(1)}, u32[]{:S(2)}, u32[]{:S(2)}) collective-permute-start(bf16[1024,4,32]{0,2,1:T(8,128)(2,1)S(1)} %slice.143), channel_id=1, source_target_pairs={{1,0},{2,1},{3,2},{4,3},{5,4},{6,5},{7,6},{9,8},{10,9},{11,10},{12... | collective-permute-start | bytes 786440 | tf_op jit(solution)/shard_map/ppermute | solution.py:30
  134.7 1.4 fusion.27
  136.5 3.3 %collective-permute-done.6 = bf16[1024,4,32]{0,2,1:T(8,128)(2,1)S(1)} collective-permute-done((bf16[1024,4,32]{0,2,1:T(8,128)(2,1)S(1)}, bf16[1024,4,32]{0,2,1:T(8,128)(2,1)S(1)}, u32[]{:S(2)}, u32[]{:S(2)}) %collective-permute-start.6) | collective-permute-done | bytes 262176 | tf_op jit(solution)/shard_map/ppermute | solution.py:30
  140.0 1.4 copy-done.2
  141.4 1.1 fusion
  142.6 1.4 fusion.26
  143.9 1.4 fusion.28
  (32 shorter events, 3.6 us)
Async XLA Ops:
  0.6 134.0 %copy-start = (bf16[1024,1024]{1,0:T(8,128)(2,1)S(1)}, bf16[1024,1024]{1,0:T(8,128)(2,1)}, u32[]{:S(2)}) copy-start(bf16[1024,1024]{1,0:T(8,128)(2,1)} %param.7) | copy-start | bytes 6291460
  1.5 26.0 %collective-permute-start = (f32[1,1024]{1,0:T(1,128)S(1)}, f32[1,1024]{1,0:T(1,128)S(1)}, u32[]{:S(2)}, u32[]{:S(2)}) collective-permute-start(f32[1,1024]{1,0:T(1,128)S(1)} %get-tuple-element.34), channel_id=1, source_target_pairs={{8,0},{16,8},{24,16},{32,24},{40,32},{48,40},{56,48},{64,56},{72,6... | collective-permute-start | bytes 12296 | tf_op jit(solution)/shard_map/ppermute | solution.py:22
  8.7 13.0 %copy-start.3 = (f32[4,1024]{1,0:T(4,128)S(1)}, f32[4,1024]{1,0:T(4,128)}, u32[]{:S(2)}) copy-start(f32[4,1024]{1,0:T(4,128)} %param.4) | copy-start | bytes 49156
  8.7 18.9 %collective-permute-start.1 = (f32[1,1024]{1,0:T(1,128)S(1)}, f32[1,1024]{1,0:T(1,128)S(1)}, u32[]{:S(2)}, u32[]{:S(2)}) collective-permute-start(f32[1,1024]{1,0:T(1,128)S(1)} %get-tuple-element.33), channel_id=1, source_target_pairs={{0,8},{8,16},{16,24},{24,32},{32,40},{40,48},{48,56},{56,64},{64,7... | collective-permute-start | bytes 12296 | tf_op jit(solution)/shard_map/ppermute | solution.py:19
  12.2 12.5 %copy-start.1 = (f32[128,4,1024]{2,0,1:T(8,128)}, f32[128,4,1024]{2,0,1:T(8,128)S(1)}, u32[]{:S(2)}) copy-start(f32[128,4,1024]{2,0,1:T(8,128)S(1)} %copy_convert_fusion) | copy-start | bytes 6291460
  13.5 16.7 %collective-permute-start.2 = (f32[128,1,1024]{2,0,1:T(8,128)}, f32[128,1,1024]{2,0,1:T(8,128)S(1)}, u32[]{:S(2)}, u32[]{:S(2)}) collective-permute-start(f32[128,1,1024]{2,0,1:T(8,128)} %get-tuple-element.25), channel_id=1, source_target_pairs={{8,0},{16,8},{24,16},{32,24},{40,32},{48,40},{56,48},{64,56},{72,6... | collective-permute-start | bytes 1572872 | tf_op jit(solution)/shard_map/ppermute | solution.py:22
  19.8 18.8 %collective-permute-start.3 = (f32[128,1,1024]{2,0,1:T(8,128)}, f32[128,1,1024]{2,0,1:T(8,128)S(1)}, u32[]{:S(2)}, u32[]{:S(2)}) collective-permute-start(f32[128,1,1024]{2,0,1:T(8,128)} %get-tuple-element.26), channel_id=1, source_target_pairs={{0,8},{8,16},{16,24},{24,32},{32,40},{40,48},{48,56},{56,64},{64,7... | collective-permute-start | bytes 1572872 | tf_op jit(solution)/shard_map/ppermute | solution.py:19
  24.7 2.8 %copy-start.4 = (s32[128,2]{0,1:T(2,128)S(1)}, s32[128,2]{0,1:T(2,128)}, u32[]{:S(2)}) copy-start(s32[128,2]{0,1:T(2,128)} %param.6) | copy-start | bytes 3076
  45.0 20.8 %collective-permute-start.4 = (f32[128,1,1024]{2,0,1:T(8,128)S(1)}, f32[128,1,1024]{2,0,1:T(8,128)S(1)}, u32[]{:S(2)}, u32[]{:S(2)}) collective-permute-start(f32[128,1,1024]{2,0,1:T(8,128)S(1)} %get-tuple-element.15), channel_id=1, source_target_pairs={{8,0},{16,8},{24,16},{32,24},{40,32},{48,40},{56,48},{64,56},{72,6... | collective-permute-start | bytes 1572872 | tf_op jit(solution)/shard_map/ppermute | solution.py:22
  55.1 17.6 %collective-permute-start.5 = (f32[128,1,1024]{2,0,1:T(8,128)S(1)}, f32[128,1,1024]{2,0,1:T(8,128)S(1)}, u32[]{:S(2)}, u32[]{:S(2)}) collective-permute-start(f32[128,1,1024]{2,0,1:T(8,128)S(1)} %get-tuple-element.16), channel_id=1, source_target_pairs={{0,8},{8,16},{16,24},{24,32},{32,40},{40,48},{48,56},{56,64},{64,7... | collective-permute-start | bytes 1572872 | tf_op jit(solution)/shard_map/ppermute | solution.py:19
  77.0 33.0 %all-to-all-start = ((bf16[128,4,1024]{0,1,2:T(4,128)(2,1)}), bf16[128,4,1024]{0,1,2:T(4,128)(2,1)}, u32[]{:S(2)}, u32[]{:S(2)}) async-start(bf16[128,4,1024]{0,1,2:T(4,128)(2,1)} %copy.12), calls=%async_computation | async-start | bytes 2097152 | tf_op jit(solution)/shard_map/all_to_all | solution.py:119
  115.8 20.5 %collective-permute-start.7 = (bf16[1024,128]{0,1:T(8,128)(2,1)S(1)}, bf16[1024,128]{0,1:T(8,128)(2,1)S(1)}, u32[]{:S(2)}, u32[]{:S(2)}) collective-permute-start(bf16[1024,128]{0,1:T(8,128)(2,1)S(1)} %slice_bitcast_fusion), channel_id=1, source_target_pairs={{8,0},{16,8},{24,16},{32,24},{40,32},{48,40},{56,48},{64,56},{72,6... | collective-permute-start | bytes 786440 | tf_op jit(solution)/shard_map/ppermute | solution.py:30
  131.2 8.6 %collective-permute-start.6 = (bf16[1024,4,32]{0,2,1:T(8,128)(2,1)S(1)}, bf16[1024,4,32]{0,2,1:T(8,128)(2,1)S(1)}, u32[]{:S(2)}, u32[]{:S(2)}) collective-permute-start(bf16[1024,4,32]{0,2,1:T(8,128)(2,1)S(1)} %slice.143), channel_id=1, source_target_pairs={{1,0},{2,1},{3,2},{4,3},{5,4},{6,5},{7,6},{9,8},{10,9},{11,10},{12... | collective-permute-start | bytes 786440 | tf_op jit(solution)/shard_map/ppermute | solution.py:30
  139.9 1.6 %copy-start.2 = (f32[8,128,4,128]{1,0,3,2:T(8,128)S(1)}, f32[8,128,4,128]{1,0,3,2:T(8,128)}, u32[]{:S(2)}) copy-start(f32[8,128,4,128]{1,0,3,2:T(8,128)} %get-tuple-element.27) | copy-start | bytes 6291460
where the time goes:
time: 146 us
  starting transfers between devices  58.8 us (40%)
  waiting for transfers between devices  48.6 us (33%)
  other arithmetic  16.8 us (12%)
  local copies, waits for them, and re-layouts  16.5 us (11%)
  matrix products  4.12 us (3%)
    ppermute x3, starting transfers between devices, with_halo(): lax.ppermute(lax.slice_in_dim(block, 0, width, axis=dim), axis, backward)  23.7 us
    all_to_all x1, waiting for transfers between devices, body(): lax.all_to_all(potentials, 'src', split_axis=2, concat_axis=0, tiled=True)  20.2 us
    ppermute x2, starting transfers between devices, shifted_2(): lax.ppermute(value, axis, [(source, source + steps) for source in range(i...  18.4 us
    ppermute x3, waiting for transfers between devices, with_halo(): lax.ppermute(lax.slice_in_dim(block, block.shape[dim] - width, None, axis...  15.4 us
    all_to_all x1, starting transfers between devices, body(): lax.all_to_all(potentials, 'src', split_axis=2, concat_axis=0, tiled=True)  11 us
    ppermute x3, waiting for transfers between devices, with_halo(): lax.ppermute(lax.slice_in_dim(block, 0, width, axis=dim), axis, backward)  9.54 us
    slice x5, local copies, waits for them, and re-layouts, shift_last(): return jnp.concatenate([values[..., offset:], padding], axis=-1)  7.59 us
    add x1, other arithmetic, relax(): return fields + relaxation * (source - applied) / diagonal  6.24 us
  transfers between devices with their start and end apart: 9, of which 7 were waited for; matrix products, arithmetic and copies ran while one was open for 10% of the time, Pallas kernels for 0%

commit v1 on v0

v1 whole, which is shorter than its diff:
```python
import jax
import jax.numpy as jnp
from jax import lax
from jax.experimental import pallas as pl
from jax.experimental.pallas import tpu as pltpu
from jax.sharding import PartitionSpec as P

NY = 32
LANES = 128
CHUNKS = 4
GROUP = 16
relaxation = 2.0 / 3.0
current = 4.0
MESH = pl.DeviceIdType.MESH


def kernel(
    cond, prev, electrodes, weight_hbm, pot, grad,
    halo, sigma_halo, coef, first, packed, gathered, partner, above, beside, weight, diffs,
    halo_send, halo_recv, sigma_send, sigma_recv, main_send, main_recv, side_send, side_recv,
    above_send, above_recv, partner_send, partner_recv, weight_sem,
):
    slabs, groups = lax.axis_size("cells"), lax.axis_size("src")
    depth, local, plane = prev.shape
    tiles = plane // LANES
    rows = local // CHUNKS
    count = groups * local
    k, j = lax.axis_index("cells"), lax.axis_index("src")
    odd = lax.rem(j, 2) == 1
    has_low, has_high = k > 0, k < slabs - 1
    sided = jnp.logical_and(odd, j < groups - 1)

    weight_copy = pltpu.make_async_copy(weight_hbm, weight, weight_sem)
    weight_copy.start()

    barrier = pltpu.get_barrier_semaphore()

    @pl.when(has_low)
    def _():
        pl.semaphore_signal(barrier, inc=1, device_id=(k - 1, j), device_id_type=MESH)

    @pl.when(has_high)
    def _():
        pl.semaphore_signal(barrier, inc=1, device_id=(k + 1, j), device_id_type=MESH)

    for r in range(1, groups):
        pl.semaphore_signal(
            barrier, inc=1, device_id=(k, lax.rem(j + r, groups)), device_id_type=MESH
        )
    pl.semaphore_wait(
        barrier, groups - 1 + has_low.astype(jnp.int32) + has_high.astype(jnp.int32)
    )

    def sigma_copy(side):
        return pltpu.make_async_remote_copy(
            src_ref=cond.at[pl.ds(2 - 2 * side, 2)],
            dst_ref=sigma_halo.at[side],
            send_sem=sigma_send.at[side],
            recv_sem=sigma_recv.at[side],
            device_id=(k + 1 - 2 * side, j),
            device_id_type=MESH,
        )

    def halo_copy(side, chunk):
        span = pl.ds(pl.multiple_of(chunk * rows, rows), rows)
        return pltpu.make_async_remote_copy(
            src_ref=prev.at[pl.ds(2 - 2 * side, 2), span],
            dst_ref=halo.at[side, :, span],
            send_sem=halo_send.at[side, chunk],
            recv_sem=halo_recv.at[side, chunk],
            device_id=(k + 1 - 2 * side, j),
            device_id_type=MESH,
        )

    def main_copy(r, chunk):
        peer = lax.rem(j + r, groups)
        span = pl.ds(pl.multiple_of(chunk * rows, rows), rows)
        band = pl.ds(pl.multiple_of(peer * LANES, LANES), LANES)
        return pltpu.make_async_remote_copy(
            src_ref=pot.at[:, span, band],
            dst_ref=gathered.at[:, j, span],
            send_sem=main_send.at[r - 1, chunk],
            recv_sem=main_recv.at[r - 1, chunk],
            device_id=(k, peer),
            device_id_type=MESH,
        )

    def side_copy(r, chunk):
        peer = lax.rem(j + r, groups)
        span = pl.ds(pl.multiple_of(chunk * rows, rows), rows)
        return pltpu.make_async_remote_copy(
            src_ref=packed.at[lax.rem(peer + 1, groups), span],
            dst_ref=beside.at[j, span],
            send_sem=side_send.at[r - 1, chunk],
            recv_sem=side_recv.at[r - 1, chunk],
            device_id=(k, peer),
            device_id_type=MESH,
        )

    def takes_side(peer):
        return jnp.logical_and(lax.rem(peer, 2) == 1, peer < groups - 1)

    def above_copy(chunk):
        span = pl.ds(pl.multiple_of(chunk * rows, rows), rows)
        return pltpu.make_async_remote_copy(
            src_ref=gathered.at[0, :, span],
            dst_ref=above.at[:, span],
            send_sem=above_send.at[chunk],
            recv_sem=above_recv.at[chunk],
            device_id=(k - 1, j),
            device_id_type=MESH,
        )

    def partner_copy(chunk):
        span = pl.ds(pl.multiple_of(chunk * rows, rows), rows)
        return pltpu.make_async_remote_copy(
            src_ref=gathered.at[:, :, span],
            dst_ref=partner.at[:, :, span],
            send_sem=partner_send.at[chunk],
            recv_sem=partner_recv.at[chunk],
            device_id=(k, lax.rem(j - 1 + groups, groups)),
            device_id_type=MESH,
        )

    sends = ((has_high, 0), (has_low, 1))
    for present, side in sends:

        @pl.when(present)
        def _(side=side):
            sigma_copy(side).start()

    for chunk in range(CHUNKS):
        for present, side in sends:

            @pl.when(present)
            def _(side=side, chunk=chunk):
                halo_copy(side, chunk).start()

    receives = ((has_low, 0), (has_high, 1))
    for present, side in receives:

        @pl.when(jnp.logical_not(present))
        def _(side=side):
            sigma_halo[side] = jnp.zeros(sigma_halo.shape[1:], sigma_halo.dtype)
            halo[side] = jnp.zeros(halo.shape[1:], halo.dtype)

        @pl.when(present)
        def _(side=side):
            sigma_copy(side).wait_recv()

    @pl.when(jnp.logical_not(has_high))
    def _():
        above[...] = jnp.zeros(above.shape, above.dtype)

    @pl.when(j == groups - 1)
    def _():
        beside[...] = jnp.zeros(beside.shape, beside.dtype)

    cell = lax.broadcasted_iota(jnp.int32, (1, plane), 1)
    column = lax.rem(cell, NY)
    own = cond[...]
    low, high = sigma_halo[0], sigma_halo[1]
    sigma = (
        [low[i : i + 1] for i in range(2)]
        + [own[i : i + 1] for i in range(depth)]
        + [high[i : i + 1] for i in range(2)]
    )
    for p in range(depth + 2):
        s, down, up = sigma[p + 1], sigma[p], sigma[p + 2]
        y_up = jnp.where(column != NY - 1, pltpu.roll(s, plane - 1, 1), 0.0)
        y_down = jnp.where(column != 0, pltpu.roll(s, 1, 1), 0.0)
        x_up = jnp.where(cell < plane - NY, pltpu.roll(s, plane - NY, 1), 0.0)
        x_down = jnp.where(cell >= NY, pltpu.roll(s, NY, 1), 0.0)
        faces = [0.5 * (s + o) for o in (up, down, y_up, y_down, x_up, x_down)]
        diagonal = faces[0] + faces[1] + faces[2] + faces[3] + faces[4] + faces[5]
        scale = relaxation / diagonal
        center = jnp.full((1, plane), 1.0 - relaxation, jnp.float32)
        if p == 0:
            scale = jnp.where(has_low, scale, 0.0)
            center = jnp.where(has_low, center, 0.0)
        if p == depth + 1:
            scale = jnp.where(has_high, scale, 0.0)
            center = jnp.where(has_high, center, 0.0)
        terms = [
            faces[0] * scale,
            faces[1] * scale,
            jnp.where(column != NY - 1, faces[2] * scale, 0.0),
            jnp.where(column != 0, faces[3] * scale, 0.0),
            jnp.where(cell < plane - NY, faces[4] * scale, 0.0),
            jnp.where(cell >= NY, faces[5] * scale, 0.0),
            center,
            current * scale,
        ]
        for i, term in enumerate(terms):
            coef[p, i : i + 1, :] = term

    lane = lax.broadcasted_iota(jnp.int32, (GROUP, LANES), 1)
    first_cell = k * (depth * plane)

    def sweep(value, p, pair, store):
        low_cell = first_cell + (p - 1) * plane
        plus, minus = pair[0] - low_cell, pair[1] - low_cell
        mids = [value(p, v) for v in range(tiles)]
        ups = [pltpu.roll(m, LANES - NY, 1) for m in mids]
        downs = [pltpu.roll(m, NY, 1) for m in mids]
        for v in range(tiles):
            c = [coef[p, i : i + 1, v * LANES : (v + 1) * LANES] for i in range(8)]
            x_up = jnp.where(lane < LANES - NY, ups[v], ups[v + 1]) if v < tiles - 1 else ups[v]
            x_down = jnp.where(lane >= NY, downs[v], downs[v - 1]) if v > 0 else downs[v]
            total = c[6] * mids[v] + c[0] * value(p + 1, v) + c[1] * value(p - 1, v)
            total = total + c[2] * pltpu.roll(mids[v], LANES - 1, 1)
            total = total + c[3] * pltpu.roll(mids[v], 1, 1)
            total = total + c[4] * x_up + c[5] * x_down
            here = lane + v * LANES
            gain = jnp.broadcast_to(c[7], (GROUP, LANES))
            total = total + jnp.where(here == plus, gain, jnp.where(here == minus, -gain, 0.0))
            store(v, total)

    def relax_group(g):
        span = pl.ds(pl.multiple_of(g * GROUP, GROUP), GROUP)
        pair = electrodes[span, :]
        pair = [
            jnp.broadcast_to(pair[:, 0:1], (GROUP, LANES)),
            jnp.broadcast_to(pair[:, 1:2], (GROUP, LANES)),
        ]

        def start(q, v):
            at = slice(v * LANES, (v + 1) * LANES)
            if q < 1:
                block = halo[0, q + 1, span, at]
            elif q <= depth:
                block = prev[q - 1, span, at]
            else:
                block = halo[1, q - depth - 1, span, at]
            return block.astype(jnp.float32)

        for p in range(depth + 2):

            def keep(v, total, p=p):
                first[p, :, v * LANES : (v + 1) * LANES] = total

            sweep(start, p, pair, keep)

        heads = [[None] * depth for _ in range(tiles)]

        def middle(q, v):
            return first[q, :, v * LANES : (v + 1) * LANES]

        for p in range(1, depth + 1):

            def keep(v, total, p=p):
                pot[p - 1, span, v * LANES : (v + 1) * LANES] = total.astype(pot.dtype)
                if v % 2 == 0:
                    turned = total if p == 1 else pltpu.roll(total, (p - 1) * NY, 1)
                    if p == 1:
                        heads[v] = turned
                    else:
                        heads[v] = jnp.where(lane < (p - 1) * NY, heads[v], turned)

            sweep(middle, p, pair, keep)
        for v in range(0, tiles, 2):
            packed[v, span] = heads[v].astype(packed.dtype)

    per_chunk = rows // GROUP

    def relax_chunk(chunk, carry):
        for present, side in receives:

            @pl.when(present)
            def _(side=side):
                halo_copy(side, chunk).wait_recv()

        def one(g, carry):
            relax_group(chunk * per_chunk + g)
            return carry

        lax.fori_loop(0, per_chunk, one, 0)
        span = pl.ds(pl.multiple_of(chunk * rows, rows), rows)
        band = pl.ds(pl.multiple_of(j * LANES, LANES), LANES)
        for p in range(depth):
            gathered[p, j, span] = pot[p, span, band]

        @pl.when(sided)
        def _():
            beside[j, span] = packed[lax.rem(j + 1, groups), span]

        for r in range(1, groups):
            main_copy(r, chunk).start()

            @pl.when(takes_side(lax.rem(j + r, groups)))
            def _(r=r):
                side_copy(r, chunk).start()

        return carry

    lax.fori_loop(0, CHUNKS, relax_chunk, 0)

    def forward_chunk(chunk, carry):
        for r in range(1, groups):
            main_copy(r, chunk).wait_recv()

            @pl.when(sided)
            def _(r=r):
                side_copy(r, chunk).wait_recv()

        @pl.when(has_low)
        def _():
            above_copy(chunk).start()

        @pl.when(odd)
        def _():
            partner_copy(chunk).start()

        return carry

    lax.fori_loop(0, CHUNKS, forward_chunk, 0)

    block = 64
    per_group = local // block
    lane = lax.broadcasted_iota(jnp.int32, (block, LANES), 1)
    inner = lax.rem(lane, NY) != NY - 1

    def each_block(step):
        def one(i, carry):
            source = i // per_group
            span = pl.ds(pl.multiple_of(lax.rem(i, per_group) * block, block), block)
            step(source, span, pl.ds(pl.multiple_of(i * block, block), block))
            return carry

        lax.fori_loop(0, groups * per_group, one, 0)

    def put(d, p, at, value):
        diffs[d, at, p * LANES : (p + 1) * LANES] = value.astype(diffs.dtype)

    def along_y(source, span, at):
        for p in range(depth):
            here = gathered[p, source, span].astype(jnp.float32)
            put(1, p, at, jnp.where(inner, pltpu.roll(here, LANES - 1, 1), 0.0) - here)

    def along_x_odd(source, span, at):
        tail = beside[source, span].astype(jnp.float32)
        for p in range(depth):
            here = gathered[p, source, span].astype(jnp.float32)
            shift = (LANES - NY - NY * p) % LANES
            edge = pltpu.roll(tail, shift, 1) if shift else tail
            turned = pltpu.roll(here, LANES - NY, 1)
            put(0, p, at, jnp.where(lane < LANES - NY, turned, edge) - here)

    def along_x_even(source, span, at):
        for p in range(depth):
            here = gathered[p, source, span].astype(jnp.float32)
            edge = pltpu.roll(partner[p, source, span].astype(jnp.float32), LANES - NY, 1)
            turned = pltpu.roll(here, LANES - NY, 1)
            put(0, p, at, jnp.where(lane < LANES - NY, turned, edge) - here)

    def along_z(source, span, at):
        here = [gathered[p, source, span].astype(jnp.float32) for p in range(depth)]
        here.append(above[source, span].astype(jnp.float32))
        for p in range(depth):
            put(2, p, at, here[p + 1] - here[p])

    step_rows = 256

    def weigh(d, total):
        def one(i, total):
            at = pl.ds(pl.multiple_of(i * step_rows, step_rows), step_rows)
            mixed = jnp.dot(weight[at, :], diffs[d], preferred_element_type=jnp.float32)
            product = mixed * diffs[d, at, :].astype(jnp.float32)
            return total + jnp.sum(product.reshape(-1, 8, depth * LANES), axis=0)

        return lax.fori_loop(0, count // step_rows, one, total)

    total = jnp.zeros((8, depth * LANES), jnp.float32)
    each_block(along_y)
    weight_copy.wait()
    total = weigh(1, total)

    @pl.when(odd)
    def _():
        each_block(along_x_odd)

    @pl.when(jnp.logical_not(odd))
    def _():
        def arrive(chunk, carry):
            partner_copy(chunk).wait_recv()
            return carry

        lax.fori_loop(0, CHUNKS, arrive, 0)
        each_block(along_x_even)

    total = weigh(0, total)

    @pl.when(has_high)
    def _():
        def arrive(chunk, carry):
            above_copy(chunk).wait_recv()
            return carry

        lax.fori_loop(0, CHUNKS, arrive, 0)

    each_block(along_z)
    total = weigh(2, total)
    summed = jnp.sum(total, axis=0, keepdims=True) * (1.0 / count)
    for p in range(depth):
        grad[p : p + 1, :] = summed[:, p * LANES : (p + 1) * LANES]

    for present, side in sends:

        @pl.when(present)
        def _(side=side):
            sigma_copy(side).wait_send()

    def drain(chunk, carry):
        for present, side in sends:

            @pl.when(present)
            def _(side=side):
                halo_copy(side, chunk).wait_send()

        for r in range(1, groups):
            main_copy(r, chunk).wait_send()

            @pl.when(takes_side(lax.rem(j + r, groups)))
            def _(r=r):
                side_copy(r, chunk).wait_send()

        @pl.when(has_low)
        def _():
            above_copy(chunk).wait_send()

        @pl.when(odd)
        def _():
            partner_copy(chunk).wait_send()

        return carry

    lax.fori_loop(0, CHUNKS, drain, 0)


def body(conductivity, prev_fields, electrodes, data_weight):
    local, depth, plane = prev_fields.shape
    groups = lax.axis_size("src")
    count = groups * local
    prev = jnp.transpose(prev_fields, (1, 0, 2))
    vmem = pl.BlockSpec(memory_space=pltpu.VMEM)
    dma = pltpu.SemaphoreType.DMA
    bf16 = jnp.bfloat16
    planes, gradient = pl.pallas_call(
        kernel,
        out_shape=(
            jax.ShapeDtypeStruct((depth, local, plane), bf16),
            jax.ShapeDtypeStruct((depth, LANES), jnp.float32),
        ),
        in_specs=[vmem, vmem, vmem, pl.BlockSpec(memory_space=pl.ANY)],
        out_specs=(vmem, vmem),
        scratch_shapes=[
            pltpu.VMEM((2, 2, local, plane), bf16),
            pltpu.VMEM((2, 2, plane), jnp.float32),
            pltpu.VMEM((depth + 2, 8, plane), jnp.float32),
            pltpu.VMEM((depth + 2, GROUP, plane), jnp.float32),
            pltpu.VMEM((groups, local, LANES), bf16),
            pltpu.VMEM((depth, groups, local, LANES), bf16),
            pltpu.VMEM((depth, groups, local, LANES), bf16),
            pltpu.VMEM((groups, local, LANES), bf16),
            pltpu.VMEM((groups, local, LANES), bf16),
            pltpu.VMEM((count, count), bf16),
            pltpu.VMEM((3, count, depth * LANES), bf16),
            dma((2, CHUNKS)),
            dma((2, CHUNKS)),
            dma((2,)),
            dma((2,)),
            dma((groups - 1, CHUNKS)),
            dma((groups - 1, CHUNKS)),
            dma((groups - 1, CHUNKS)),
            dma((groups - 1, CHUNKS)),
            dma((CHUNKS,)),
            dma((CHUNKS,)),
            dma((CHUNKS,)),
            dma((CHUNKS,)),
            dma(()),
        ],
        compiler_params=pltpu.CompilerParams(
            collective_id=0, has_side_effects=True, vmem_limit_bytes=48 * 1024 * 1024
        ),
        name="step",
    )(conductivity, prev, electrodes, data_weight)
    return jnp.transpose(planes, (1, 0, 2)), gradient


def solution(mesh):
    placed = (P("cells", None), P("src", "cells", None), P("src", None), P())
    return jax.shard_map(
        body,
        mesh=mesh,
        in_specs=placed,
        out_specs=(P("src", "cells", None), P("cells", "src")),
        check_vma=False,
    )
```

time: 146 us -> 80.3 us (0.55)
  the two profiles are of different devices: /device:TPU:7 before, /device:TPU:49 now
where the time goes in v1:
time: 80.3 us; the launch traced here: 80.2 us
  Pallas kernels  74.7 us (93%)
  local copies, waits for them, and re-layouts  4.83 us (6%)
    pallas_call x1, Pallas kernels, body(): pl.pallas_call(kernel, out_shape=(jax.ShapeDtypeStruct((depth, local, pla...  74.7 us
    unnamed x8, local copies, waits for them, and re-layouts  4.83 us

profile of v1, /device:TPU:49, one launch (start us, length us, event | category | flops | bytes accessed | tf_op | source)
XLA Modules:
  0.0 80.2 jit_solution(11419384781480183037)
XLA Ops:
  0.6 0.0 copy-start
  0.6 0.0 copy-start.1
  0.6 0.9 %copy.7.electrodes = s32[128,2]{1,0:T(8,128)S(1)} copy(s32[128,2]{0,1:T(2,128)} %param.6) | data formatting | bytes 2048 | tf_op args[2]
  1.6 1.5 %copy.10 = bf16[128,4,1024]{2,0,1:T(8,128)(2,1)S(1)} copy(bf16[128,4,1024]{2,1,0:T(4,128)(2,1)} %param.5) | data formatting | bytes 2097152 | tf_op args[1]
  3.1 0.0 copy-done
  3.1 0.0 copy-done.1
  3.1 74.7 %step.1 = (bf16[4,128,1024]{2,1,0:T(8,128)(2,1)S(1)}, f32[4,128]{1,0:T(4,128)S(1)}) custom-call(f32[4,1024]{1,0:T(4,128)S(1)} %copy-done.1, bf16[4,128,1024]{2,1,0:T(8,128)(2,1)S(1)} %bitcast.4, s32[128,2]{1,0:T(8,128)S(1)} %copy.7.electrodes, bf16[1024,1024]{1,0:T(8,128)(2,1)S(1)} %copy-done), custom_call_target="tpu_custom_call" | custom-call | tf_op jit(solution)/shard_map/step/pallas_call | solution.py:448
  77.8 1.8 %copy.8 = bf16[128,4,1024]{2,1,0:T(4,128)(2,1)} copy(bf16[128,4,1024]{2,0,1:T(8,128)(2,1)S(1)} %bitcast.5) | data formatting | bytes 2097152
  79.6 0.6 copy.12
Async XLA Ops:
  0.6 2.5 %copy-start = (bf16[1024,1024]{1,0:T(8,128)(2,1)S(1)}, bf16[1024,1024]{1,0:T(8,128)(2,1)}, u32[]{:S(2)}) copy-start(bf16[1024,1024]{1,0:T(8,128)(2,1)} %weight_hbm.1) | copy-start | bytes 6291460
  0.6 2.5 %copy-start.1 = (f32[4,1024]{1,0:T(4,128)S(1)}, f32[4,1024]{1,0:T(4,128)}, u32[]{:S(2)}) copy-start(f32[4,1024]{1,0:T(4,128)} %cond.1) | copy-start | bytes 49156

commit v2 on v1

--- a/solution.py
+++ b/solution.py
@@ -11,14 +11,16 @@
 GROUP = 16
 relaxation = 2.0 / 3.0
 current = 4.0
+ORDER = (1, 2, 3, 4, 5, 6, 7)
 MESH = pl.DeviceIdType.MESH
 
 
 def kernel(
-    cond, prev, electrodes, weight_hbm, pot, grad,
-    halo, sigma_halo, coef, first, packed, gathered, partner, above, beside, weight, diffs,
-    halo_send, halo_recv, sigma_send, sigma_recv, main_send, main_recv, side_send, side_recv,
-    above_send, above_recv, partner_send, partner_recv, weight_sem,
+    cond, prev, pairs, weight, pot, grad,
+    halo, sigma_halo, coef, first, packed, gathered, partner, above, beside, electrodes, mixing,
+    diffs,
+    halo_send, halo_recv, sigma_send, sigma_recv, base_send, base_recv, main_send, main_recv,
+    side_send, side_recv, above_send, above_recv, partner_send, partner_recv,
 ):
     slabs, groups = lax.axis_size("cells"), lax.axis_size("src")
     depth, local, plane = prev.shape
@@ -30,9 +32,6 @@
     has_low, has_high = k > 0, k < slabs - 1
     sided = jnp.logical_and(odd, j < groups - 1)
 
-    weight_copy = pltpu.make_async_copy(weight_hbm, weight, weight_sem)
-    weight_copy.start()
-
     barrier = pltpu.get_barrier_semaphore()
 
     @pl.when(has_low)
@@ -72,13 +71,26 @@
             device_id_type=MESH,
         )
 
+    def base_copy(r, chunk):
+        peer = lax.rem(j + r, groups)
+        span = pl.ds(pl.multiple_of(chunk * rows, rows), rows)
+        band = pl.ds(pl.multiple_of(peer * LANES, LANES), LANES)
+        return pltpu.make_async_remote_copy(
+            src_ref=pot.at[0, span, band],
+            dst_ref=gathered.at[0, j, span],
+            send_sem=base_send.at[r - 1, chunk],
+            recv_sem=base_recv.at[r - 1, chunk],
+            device_id=(k, peer),
+            device_id_type=MESH,
+        )
+
     def main_copy(r, chunk):
         peer = lax.rem(j + r, groups)
         span = pl.ds(pl.multiple_of(chunk * rows, rows), rows)
         band = pl.ds(pl.multiple_of(peer * LANES, LANES), LANES)
         return pltpu.make_async_remote_copy(
-            src_ref=pot.at[:, span, band],
-            dst_ref=gathered.at[:, j, span],
+            src_ref=pot.at[pl.ds(1, depth - 1), span, band],
+            dst_ref=gathered.at[pl.ds(1, depth - 1), j, span],
             send_sem=main_send.at[r - 1, chunk],
             recv_sem=main_recv.at[r - 1, chunk],
             device_id=(k, peer),
@@ -135,6 +147,42 @@
             @pl.when(present)
             def _(side=side, chunk=chunk):
                 halo_copy(side, chunk).start()
+
+    wide = jnp.concatenate([pairs[...], jnp.zeros((6, local), jnp.int32)], axis=0)
+    electrodes[...] = jnp.transpose(wide)
+    quarter = lax.broadcasted_iota(jnp.int32, (rows, LANES), 1) // rows
+
+    def reorder(source, carry):
+        for chunk in range(CHUNKS):
+            at = pl.multiple_of(source * local + chunk * rows, rows)
+            turned = []
+            for other in range(groups):
+                block = weight[pl.ds(at, rows), other * LANES : (other + 1) * LANES]
+                block = block.astype(jnp.float32)
+                turned.append(
+                    [block]
+                    + [pltpu.roll(block, step * rows, 1) for step in range(1, CHUNKS)]
+                )
+            to = pl.ds(pl.multiple_of(chunk * groups * rows + source * rows, rows), rows)
+            for part in range(CHUNKS):
+                for half in range(groups // CHUNKS):
+                    q = [turned[half * CHUNKS + i][(i - part) % CHUNKS] for i in range(CHUNKS)]
+                    value = q[0]
+                    for i in range(1, CHUNKS):
+                        value = jnp.where(quarter == i, q[i], value)
+                    tile = part * (groups // CHUNKS) + half
+                    mixing[to, tile * LANES : (tile + 1) * LANES] = value.astype(mixing.dtype)
+        return carry
+
+    lax.fori_loop(0, groups, reorder, 0)
+    for chunk in range(1, CHUNKS):
+        at = slice(chunk * groups * rows, (chunk + 1) * groups * rows)
+        for other in range(chunk):
+            to = slice(other * groups * rows, (other + 1) * groups * rows)
+            both = mixing[at, to].astype(jnp.float32) + jnp.transpose(
+                mixing[to, at].astype(jnp.float32)
+            )
+            mixing[at, to] = both.astype(mixing.dtype)
 
     receives = ((has_low, 0), (has_high, 1))
     for present, side in receives:
@@ -284,18 +332,82 @@
         def _():
             beside[j, span] = packed[lax.rem(j + 1, groups), span]
 
-        for r in range(1, groups):
+        for r in ORDER:
+            base_copy(r, chunk).start()
+
+        send_rest(chunk)
+        return carry
+
+    def send_rest(chunk):
+        for r in ORDER:
             main_copy(r, chunk).start()
 
             @pl.when(takes_side(lax.rem(j + r, groups)))
             def _(r=r):
                 side_copy(r, chunk).start()
 
-        return carry
-
     lax.fori_loop(0, CHUNKS, relax_chunk, 0)
 
-    def forward_chunk(chunk, carry):
+    def raise_base(chunk):
+        for r in range(1, groups):
+            base_copy(r, chunk).wait_recv()
+
+        @pl.when(has_low)
+        def _():
+            above_copy(chunk).start()
+
+
+    early = (2 * depth - 1) * LANES
+    width = 3 * depth * LANES
+    span_rows = groups * rows
+    lane = lax.broadcasted_iota(jnp.int32, (rows, LANES), 1)
+    inner = lax.rem(lane, NY) != NY - 1
+    within = lane < LANES - NY
+
+    def each_source(chunk, step):
+        span = pl.ds(pl.multiple_of(chunk * rows, rows), rows)
+
+        def one(source, carry):
+            at = pl.ds(pl.multiple_of(chunk * span_rows + source * rows, rows), rows)
+            step(source, span, at)
+            return carry
+
+        lax.fori_loop(0, groups, one, 0)
+
+    def put(at, column, value):
+        diffs[at, column * LANES : (column + 1) * LANES] = value.astype(diffs.dtype)
+
+    def along_yz(source, span, at):
+        here = [gathered[p, source, span].astype(jnp.float32) for p in range(depth)]
+        for p in range(depth):
+            put(at, p, jnp.where(inner, pltpu.roll(here[p], LANES - 1, 1), 0.0) - here[p])
+        for p in range(depth - 1):
+            put(at, depth + p, here[p + 1] - here[p])
+
+    def along_x(source, span, at, edges):
+        for p in range(depth):
+            here = gathered[p, source, span].astype(jnp.float32)
+            turned = pltpu.roll(here, LANES - NY, 1)
+            put(at, 2 * depth - 1 + p, jnp.where(within, turned, edges(p)) - here)
+        top = above[source, span].astype(jnp.float32)
+        put(at, 3 * depth - 1, top - gathered[depth - 1, source, span].astype(jnp.float32))
+
+    def along_x_odd(source, span, at):
+        tail = beside[source, span].astype(jnp.float32)
+
+        def edges(p):
+            shift = (LANES - NY - NY * p) % LANES
+            return pltpu.roll(tail, shift, 1) if shift else tail
+
+        along_x(source, span, at, edges)
+
+    def along_x_even(source, span, at):
+        def edges(p):
+            return pltpu.roll(partner[p, source, span].astype(jnp.float32), LANES - NY, 1)
+
+        along_x(source, span, at, edges)
+
+    def take_rest(chunk):
         for r in range(1, groups):
             main_copy(r, chunk).wait_recv()
 
@@ -303,106 +415,57 @@
             def _(r=r):
                 side_copy(r, chunk).wait_recv()
 
-        @pl.when(has_low)
-        def _():
-            above_copy(chunk).start()
-
         @pl.when(odd)
         def _():
             partner_copy(chunk).start()
 
-        return carry
-
-    lax.fori_loop(0, CHUNKS, forward_chunk, 0)
-
-    block = 64
-    per_group = local // block
-    lane = lax.broadcasted_iota(jnp.int32, (block, LANES), 1)
-    inner = lax.rem(lane, NY) != NY - 1
-
-    def each_block(step):
-        def one(i, carry):
-            source = i // per_group
-            span = pl.ds(pl.multiple_of(lax.rem(i, per_group) * block, block), block)
-            step(source, span, pl.ds(pl.multiple_of(i * block, block), block))
-            return carry
-
-        lax.fori_loop(0, groups * per_group, one, 0)
-
-    def put(d, p, at, value):
-        diffs[d, at, p * LANES : (p + 1) * LANES] = value.astype(diffs.dtype)
-
-    def along_y(source, span, at):
-        for p in range(depth):
-            here = gathered[p, source, span].astype(jnp.float32)
-            put(1, p, at, jnp.where(inner, pltpu.roll(here, LANES - 1, 1), 0.0) - here)
-
-    def along_x_odd(source, span, at):
-        tail = beside[source, span].astype(jnp.float32)
-        for p in range(depth):
-            here = gathered[p, source, span].astype(jnp.float32)
-            shift = (LANES - NY - NY * p) % LANES
-            edge = pltpu.roll(tail, shift, 1) if shift else tail
-            turned = pltpu.roll(here, LANES - NY, 1)
-            put(0, p, at, jnp.where(lane < LANES - NY, turned, edge) - here)
-
-    def along_x_even(source, span, at):
-        for p in range(depth):
-            here = gathered[p, source, span].astype(jnp.float32)
-            edge = pltpu.roll(partner[p, source, span].astype(jnp.float32), LANES - NY, 1)
-            turned = pltpu.roll(here, LANES - NY, 1)
-            put(0, p, at, jnp.where(lane < LANES - NY, turned, edge) - here)
-
-    def along_z(source, span, at):
-        here = [gathered[p, source, span].astype(jnp.float32) for p in range(depth)]
-        here.append(above[source, span].astype(jnp.float32))
-        for p in range(depth):
-            put(2, p, at, here[p + 1] - here[p])
-
-    step_rows = 256
-
-    def weigh(d, total):
-        def one(i, total):
-            at = pl.ds(pl.multiple_of(i * step_rows, step_rows), step_rows)
-            mixed = jnp.dot(weight[at, :], diffs[d], preferred_element_type=jnp.float32)
-            product = mixed * diffs[d, at, :].astype(jnp.float32)
-            return total + jnp.sum(product.reshape(-1, 8, depth * LANES), axis=0)
-
-        return lax.fori_loop(0, count // step_rows, one, total)
-
-    total = jnp.zeros((8, depth * LANES), jnp.float32)
-    each_block(along_y)
-    weight_copy.wait()
-    total = weigh(1, total)
-
-    @pl.when(odd)
-    def _():
-        each_block(along_x_odd)
-
-    @pl.when(jnp.logical_not(odd))
-    def _():
-        def arrive(chunk, carry):
+        each_source(chunk, along_yz)
+
+    def take_edges(chunk):
+        @pl.when(has_high)
+        def _():
+            above_copy(chunk).wait_recv()
+
+        @pl.when(odd)
+        def _():
+            each_source(chunk, along_x_odd)
+
+        @pl.when(jnp.logical_not(odd))
+        def _():
             partner_copy(chunk).wait_recv()
-            return carry
-
-        lax.fori_loop(0, CHUNKS, arrive, 0)
-        each_block(along_x_even)
-
-    total = weigh(0, total)
-
-    @pl.when(has_high)
-    def _():
-        def arrive(chunk, carry):
-            above_copy(chunk).wait_recv()
-            return carry
-
-        lax.fori_loop(0, CHUNKS, arrive, 0)
-
-    each_block(along_z)
-    total = weigh(2, total)
-    summed = jnp.sum(total, axis=0, keepdims=True) * (1.0 / count)
+            each_source(chunk, along_x_even)
+
+    def weigh(chunk, low, high):
+        at = slice(chunk * span_rows, (chunk + 1) * span_rows)
+        reach = slice(0, (chunk + 1) * span_rows)
+        value = jnp.dot(
+            mixing[at, reach], diffs[reach, low:high], preferred_element_type=jnp.float32
+        )
+        value = value * diffs[at, low:high].astype(jnp.float32)
+        return jnp.sum(value.reshape(-1, 8, high - low), axis=0)
+
+    inside = jnp.zeros((8, early), jnp.float32)
+    outside = jnp.zeros((8, width - early), jnp.float32)
+    for chunk in range(CHUNKS - 1):
+        raise_base(chunk)
+        take_rest(chunk)
+        inside = inside + weigh(chunk, 0, early)
+    raise_base(CHUNKS - 1)
+    for chunk in range(CHUNKS - 2):
+        take_edges(chunk)
+        outside = outside + weigh(chunk, early, width)
+    take_rest(CHUNKS - 1)
+    inside = inside + weigh(CHUNKS - 1, 0, early)
+    for chunk in (CHUNKS - 2, CHUNKS - 1):
+        take_edges(chunk)
+        outside = outside + weigh(chunk, early, width)
+    inside = jnp.sum(inside, axis=0, keepdims=True) * (1.0 / count)
+    outside = jnp.sum(outside, axis=0, keepdims=True) * (1.0 / count)
+    columns = [inside[:, i * LANES : (i + 1) * LANES] for i in range(2 * depth - 1)]
+    columns += [outside[:, i * LANES : (i + 1) * LANES] for i in range(depth + 1)]
     for p in range(depth):
-        grad[p : p + 1, :] = summed[:, p * LANES : (p + 1) * LANES]
+        last = columns[depth + p] if p < depth - 1 else columns[3 * depth - 1]
+        grad[p : p + 1, :] = columns[p] + columns[2 * depth - 1 + p] + last
 
     for present, side in sends:
 
@@ -418,6 +481,7 @@
                 halo_copy(side, chunk).wait_send()
 
         for r in range(1, groups):
+            base_copy(r, chunk).wait_send()
             main_copy(r, chunk).wait_send()
 
             @pl.when(takes_side(lax.rem(j + r, groups)))
@@ -451,7 +515,7 @@
             jax.ShapeDtypeStruct((depth, local, plane), bf16),
             jax.ShapeDtypeStruct((depth, LANES), jnp.float32),
         ),
-        in_specs=[vmem, vmem, vmem, pl.BlockSpec(memory_space=pl.ANY)],
+        in_specs=[vmem] * 4,
         out_specs=(vmem, vmem),
         scratch_shapes=[
             pltpu.VMEM((2, 2, local, plane), bf16),
@@ -463,8 +527,9 @@
             pltpu.VMEM((depth, groups, local, LANES), bf16),
             pltpu.VMEM((groups, local, LANES), bf16),
             pltpu.VMEM((groups, local, LANES), bf16),
+            pltpu.VMEM((local, 8), jnp.int32),
             pltpu.VMEM((count, count), bf16),
-            pltpu.VMEM((3, count, depth * LANES), bf16),
+            pltpu.VMEM((count, 3 * depth * LANES), bf16),
             dma((2, CHUNKS)),
             dma((2, CHUNKS)),
             dma((2,)),
@@ -473,17 +538,18 @@
             dma((groups - 1, CHUNKS)),
             dma((groups - 1, CHUNKS)),
             dma((groups - 1, CHUNKS)),
+            dma((groups - 1, CHUNKS)),
+            dma((groups - 1, CHUNKS)),
             dma((CHUNKS,)),
             dma((CHUNKS,)),
             dma((CHUNKS,)),
             dma((CHUNKS,)),
-            dma(()),
         ],
         compiler_params=pltpu.CompilerParams(
             collective_id=0, has_side_effects=True, vmem_limit_bytes=48 * 1024 * 1024
         ),
         name="step",
-    )(conductivity, prev, electrodes, data_weight)
+    )(conductivity, prev, jnp.transpose(electrodes), data_weight)
     return jnp.transpose(planes, (1, 0, 2)), gradient
 
 

time: 80.3 us -> 76.5 us (0.953)
  the two profiles are of different devices: /device:TPU:49 before, /device:TPU:7 now
where the time goes in v2:
time: 76.5 us; the launch traced here: 75.6 us
  Pallas kernels  70 us (92%)
  local copies, waits for them, and re-layouts  4.96 us (6%)
    pallas_call x1, Pallas kernels, body(): pl.pallas_call(kernel, out_shape=(jax.ShapeDtypeStruct((depth, local, pla...  70 us
    unnamed x9, local copies, waits for them, and re-layouts  4.96 us

profile of v2, /device:TPU:7, one launch (start us, length us, event | category | flops | bytes accessed | tf_op | source)
XLA Modules:
  0.0 75.6 jit_solution(5748057615850726850)
XLA Ops:
  0.6 0.0 copy-start
  0.6 0.0 copy-start.2
  0.7 1.7 %copy.9 = bf16[128,4,1024]{2,0,1:T(8,128)(2,1)S(1)} copy(bf16[128,4,1024]{2,1,0:T(4,128)(2,1)} %param.5) | data formatting | bytes 2097152 | tf_op args[1]
  2.3 0.2 copy-done
  2.5 0.0 copy-done.2
  2.5 0.0 copy-start.1
  2.5 0.7 copy-done.1
  3.3 70.0 %step.1 = (bf16[4,128,1024]{2,1,0:T(8,128)(2,1)S(1)}, f32[4,128]{1,0:T(4,128)S(1)}) custom-call(f32[4,1024]{1,0:T(4,128)S(1)} %copy-done.1, bf16[4,128,1024]{2,1,0:T(8,128)(2,1)S(1)} %bitcast.5, s32[2,128]{1,0:T(2,128)S(1)} %bitcast.7, bf16[1024,1024]{1,0:T(8,128)(2,1)S(1)} %copy-done), custom_call_target="tpu_custom_call" | custom-call | tf_op jit(solution)/shard_map/step/pallas_call | solution.py:512
  73.2 1.8 %copy.7 = bf16[128,4,1024]{2,1,0:T(4,128)(2,1)} copy(bf16[128,4,1024]{2,0,1:T(8,128)(2,1)S(1)} %bitcast.6) | data formatting | bytes 2097152
  75.0 0.6 copy.11
Async XLA Ops:
  0.6 1.9 %copy-start = (bf16[1024,1024]{1,0:T(8,128)(2,1)S(1)}, bf16[1024,1024]{1,0:T(8,128)(2,1)}, u32[]{:S(2)}) copy-start(bf16[1024,1024]{1,0:T(8,128)(2,1)} %weight.1) | copy-start | bytes 6291460
  0.6 1.9 %copy-start.2 = (s32[128,2]{0,1:T(2,128)S(1)}, s32[128,2]{0,1:T(2,128)}, u32[]{:S(2)}) copy-start(s32[128,2]{0,1:T(2,128)} %param.6) | copy-start | bytes 3076
  2.5 0.7 copy-start.1

commit v3 on v2

--- a/solution.py
+++ b/solution.py
@@ -16,9 +16,9 @@
 
 
 def kernel(
-    cond, prev, pairs, weight, pot, grad,
+    cond_hbm, prev, pairs, weight, out, grad,
     halo, sigma_halo, coef, first, packed, gathered, partner, above, beside, electrodes, mixing,
-    diffs,
+    diffs, pot, cond, cond_sem,
     halo_send, halo_recv, sigma_send, sigma_recv, base_send, base_recv, main_send, main_recv,
     side_send, side_recv, above_send, above_recv, partner_send, partner_recv,
 ):
@@ -32,6 +32,9 @@
     has_low, has_high = k > 0, k < slabs - 1
     sided = jnp.logical_and(odd, j < groups - 1)
 
+    cond_copy = pltpu.make_async_copy(cond_hbm, cond, cond_sem)
+    cond_copy.start()
+
     barrier = pltpu.get_barrier_semaphore()
 
     @pl.when(has_low)
@@ -52,7 +55,7 @@
 
     def sigma_copy(side):
         return pltpu.make_async_remote_copy(
-            src_ref=cond.at[pl.ds(2 - 2 * side, 2)],
+            src_ref=cond_hbm.at[pl.ds(2 - 2 * side, 2)],
             dst_ref=sigma_halo.at[side],
             send_sem=sigma_send.at[side],
             recv_sem=sigma_recv.at[side],
@@ -206,6 +209,7 @@
 
     cell = lax.broadcasted_iota(jnp.int32, (1, plane), 1)
     column = lax.rem(cell, NY)
+    cond_copy.wait()
     own = cond[...]
     low, high = sigma_halo[0], sigma_halo[1]
     sigma = (
@@ -348,6 +352,16 @@
 
     lax.fori_loop(0, CHUNKS, relax_chunk, 0)
 
+    def regroup(g, carry):
+        span = pl.ds(pl.multiple_of(g * GROUP, GROUP), GROUP)
+        for v in range(tiles):
+            at = slice(v * LANES, (v + 1) * LANES)
+            parts = [pot[p, span, at].astype(jnp.float32) for p in range(depth)]
+            out[span, :, at] = jnp.stack(parts, axis=1).astype(out.dtype)
+        return carry
+
+    lax.fori_loop(0, local // GROUP, regroup, 0)
+
     def raise_base(chunk):
         for r in range(1, groups):
             base_copy(r, chunk).wait_recv()
@@ -509,13 +523,13 @@
     vmem = pl.BlockSpec(memory_space=pltpu.VMEM)
     dma = pltpu.SemaphoreType.DMA
     bf16 = jnp.bfloat16
-    planes, gradient = pl.pallas_call(
+    return pl.pallas_call(
         kernel,
         out_shape=(
-            jax.ShapeDtypeStruct((depth, local, plane), bf16),
+            jax.ShapeDtypeStruct((local, depth, plane), bf16),
             jax.ShapeDtypeStruct((depth, LANES), jnp.float32),
         ),
-        in_specs=[vmem] * 4,
+        in_specs=[pl.BlockSpec(memory_space=pltpu.HBM), vmem, vmem, vmem],
         out_specs=(vmem, vmem),
         scratch_shapes=[
             pltpu.VMEM((2, 2, local, plane), bf16),
@@ -530,6 +544,9 @@
             pltpu.VMEM((local, 8), jnp.int32),
             pltpu.VMEM((count, count), bf16),
             pltpu.VMEM((count, 3 * depth * LANES), bf16),
+            pltpu.VMEM((depth, local, plane), bf16),
+            pltpu.VMEM((depth, plane), jnp.float32),
+            dma(()),
             dma((2, CHUNKS)),
             dma((2, CHUNKS)),
             dma((2,)),
@@ -549,8 +566,12 @@
             collective_id=0, has_side_effects=True, vmem_limit_bytes=48 * 1024 * 1024
         ),
         name="step",
-    )(conductivity, prev, jnp.transpose(electrodes), data_weight)
-    return jnp.transpose(planes, (1, 0, 2)), gradient
+    )(
+        pltpu.with_memory_space_constraint(conductivity, pltpu.HBM),
+        prev,
+        jnp.transpose(electrodes),
+        data_weight,
+    )
 
 
 def solution(mesh):

time: 76.5 us -> 75.1 us (0.982)
  local copies, waits for them, and re-layouts: 4.96 us -> 3.44 us
    unnamed x9 -> x7, local copies, waits for them, and re-layouts: 4.96 us -> 3.44 us
where the time goes in v3:
time: 75.1 us; the launch traced here: 74.3 us
  Pallas kernels  70.2 us (93%)
  local copies, waits for them, and re-layouts  3.44 us (5%)
    pallas_call x1, Pallas kernels, body(): pl.pallas_call(kernel, out_shape=(jax.ShapeDtypeStruct((local, depth, pla...  70.2 us
    unnamed x7, local copies, waits for them, and re-layouts  3.44 us

profile of v3, /device:TPU:7, one launch (start us, length us, event | category | flops | bytes accessed | tf_op | source)
XLA Modules:
  0.0 74.3 jit_solution(16607374538639020075)
XLA Ops:
  0.6 0.0 copy-start
  0.6 0.0 copy-start.1
  0.7 1.7 %copy.8 = bf16[128,4,1024]{2,0,1:T(8,128)(2,1)S(1)} copy(bf16[128,4,1024]{2,1,0:T(4,128)(2,1)} %param.5) | data formatting | bytes 2097152 | tf_op args[1]
  2.3 0.2 copy-done
  2.5 0.0 copy-done.1
  2.5 70.2 %step.1 = (bf16[128,4,1024]{2,1,0:T(4,128)(2,1)S(1)}, f32[4,128]{1,0:T(4,128)S(1)}) custom-call(f32[4,1024]{1,0:T(4,128)} %cond_hbm.1, bf16[4,128,1024]{2,1,0:T(8,128)(2,1)S(1)} %bitcast.4, s32[2,128]{1,0:T(2,128)S(1)} %bitcast.5, bf16[1024,1024]{1,0:T(8,128)(2,1)S(1)} %copy-done), custom_call_target="tpu_custom_call" | custom-call | tf_op jit(solution)/shard_map/step/pallas_call | solution.py:526
  72.8 1.0 %copy.11 = bf16[128,4,1024]{2,1,0:T(4,128)(2,1)} copy(bf16[128,4,1024]{2,1,0:T(4,128)(2,1)S(1)} %get-tuple-element.4) | data formatting | bytes 2097152
  73.7 0.6 copy.12
Async XLA Ops:
  0.6 1.9 %copy-start = (bf16[1024,1024]{1,0:T(8,128)(2,1)S(1)}, bf16[1024,1024]{1,0:T(8,128)(2,1)}, u32[]{:S(2)}) copy-start(bf16[1024,1024]{1,0:T(8,128)(2,1)} %weight.1) | copy-start | bytes 6291460
  0.6 1.9 %copy-start.1 = (s32[128,2]{0,1:T(2,128)S(1)}, s32[128,2]{0,1:T(2,128)}, u32[]{:S(2)}) copy-start(s32[128,2]{0,1:T(2,128)} %param.6) | copy-start | bytes 3076
